TPU v7x, 32 devices: a whole 2x2x4 slice. The times are simulated.
32 devices in a mesh: mkt: 4 (over z), prod: 2 (over core), draw: 4 (over y, x).
Axes of the slice: x: 2, y: 2, z: 4, core: 2. Of those that a mesh axis runs over, the one named last changes fastest.
Arguments:
- start_utility: float32 [1024, 256], P('mkt', 'prod'), may hold values from -5 to -2
- log_shares: float32 [1024, 256], P('mkt', 'prod'), may hold values from -9 to -5
- characteristics: float32 [1024, 8, 256], P('mkt', None, 'prod'), may hold values from -2.5 to 2.5
- coef_scale: float32 [8], replicated, may hold values from 0.1 to 0.3
- taste_draws: float32 [1024, 8, 2048], P('mkt', None, 'draw'), may hold values from -2.5 to 2.5
Outputs:
- mean_utility: float32 [1024, 256], P('mkt', 'prod')
- step_norms: float32 [2], replicated
All inputs are finite; a program needn't handle non-finite values.
Results may differ from a plain program's by a relative error of at most 0.0001.
Values sent between devices are 32-bit elements; how exact they have to be, the bound alone decides.
A program may use at most 64 MiB of HBM per device.

v0:
```python
import math

import jax
import jax.numpy as jnp
from jax import lax
from jax.sharding import PartitionSpec as P

R = 2048
ITERS = 2


def exponent(chars_part, scaled_part, util_part):
    spread = jnp.einsum("mkj,mkr->mjr", chars_part, scaled_part, precision=lax.Precision.HIGHEST)
    return jnp.exp(util_part[:, :, None] + spread)


def shards(start_utility, log_shares, characteristics, coef_scale, taste_draws):
    markets, coef_count, local_prod = characteristics.shape
    local_draws = taste_draws.shape[2]
    scaled = taste_draws * coef_scale[None, :, None]
    block_size = math.gcd(markets, 32)
    block_count = markets // block_size
    scaled_blocks = scaled.reshape(block_count, block_size, coef_count, local_draws)
    all_chars = lax.all_gather(characteristics, "prod", axis=2, tiled=True)
    all_blocks = all_chars.reshape(block_count, block_size, coef_count, -1)
    offset = lax.axis_index("prod") * local_prod
    utility = start_utility
    norm_list = []
    for iteration in range(ITERS):
        full_utility = lax.all_gather(utility, "prod", axis=1, tiled=True)

        def whole_pass(inputs):
            chars_part, scaled_part, util_part = inputs
            exp_util = exponent(chars_part, scaled_part, util_part)
            denominator = 1.0 + jnp.sum(exp_util, axis=1, keepdims=True)
            own_part = lax.dynamic_slice_in_dim(exp_util, offset, local_prod, 1)
            return jnp.sum(own_part / denominator, axis=2)

        summed = lax.map(
            whole_pass,
            (all_blocks, scaled_blocks, full_utility.reshape(block_count, block_size, -1)),
        )
        predicted = lax.psum(summed.reshape(markets, local_prod), "draw") / R
        updated = utility + log_shares - jnp.log(predicted)
        change = updated - utility
        square_sum = jnp.sum(change * change)
        norm_list.append(lax.psum(square_sum, ("mkt", "prod")))
        utility = updated
    totals = jnp.stack(norm_list)
    cell_count = markets * local_prod * lax.axis_size("mkt") * lax.axis_size("prod")
    step_norms = jnp.sqrt(totals / cell_count + 1e-06)
    return (utility, step_norms)


def solution(mesh):
    return jax.shard_map(
        shards,
        mesh=mesh,
        in_specs=(
            P("mkt", "prod"),
            P("mkt", "prod"),
            P("mkt", None, "prod"),
            P(),
            P("mkt", None, "draw"),
        ),
        out_specs=(P("mkt", "prod"), P()),
        check_vma=False,
    )
```

profile of v0, /device:TPU:0, one launch (start us, length us, event | category | flops | bytes accessed | tf_op | source)
XLA Modules:
  0.0 413.3 jit_solution(8134202163170635806)
XLA Ops:
  7.2 0.7 all-gather.2.cloned.1.call-update
  7.9 2.3 all_gather.9
  10.3 4.7 %broadcast_multiply_fusion = f32[256,8,512]{2,1,0:T(8,128)} fusion(f32[256,8,512]{2,1,0:T(8,128)} %param.13, f32[8]{0:T(128)} %param.12), kind=kLoop, calls=%fused_computation.22 | loop fusion | flops 1048576 | bytes 8388640 | tf_op jit(solution)/shard_map/mul | solution.py:20
  15.0 7.4 %all-gather.2.cloned.1.call-done = f32[256,8,256]{2,1,0:T(8,128)} async-done(((f32[256,8,128]{2,1,0:T(8,128)}), f32[256,8,256]{2,1,0:T(8,128)}) %all-gather.2.cloned.1.call-update) | async-done | bytes 2097168 | tf_op jit(solution)/shard_map/all_gather | solution.py:24
  22.4 136.7 %while.24 = (s32[]{:T(128)}, f32[8,32,128]{2,1,0:T(8,128)S(1)}, f32[8,32,256]{2,1,0:T(8,128)S(1)}, f32[8,32,8,256]{3,2,1,0:T(8,128)}, f32[8,32,8,512]{3,2,1,0:T(8,128)}, /*index=5*/s32[]{:T(128)}, s32[]{:T(128)}) while((s32[]{:T(128)}, f32[8,32,128]{2,1,0:T(8,128)S(1)}, f32[8,32,256]{2,1,0:T(8,128)S(1)}, f32[8,32,8,256]{3,2,1,0:T(8,128)}, ...), condition=%wide.region_3.4_spmd, body=%wide.region_0.3_spmd.sunk | while | flops 415232000 | bytes 26362968 | solution.py:39
  22.4 16.4 %fusion.20 = (f32[32,512]{1,0:T(8,128)S(1)}, f32[32,256,512]{2,1,0:T(8,128)S(1)}) fusion(f32[8,32,8,512]{3,2,1,0:T(8,128)} %get-tuple-element.285, s32[]{:T(128)} %get-tuple-element.274, f32[8,32,8,256]{3,2,1,0:T(8,128)} %get-tuple-element.284, f32[32,256]{1,0:T(8,128)S(1)} %dynamic-slice_bitcast_fusion.4), kind=kOutput, calls=%fused_computation.30.clone.1 | convolution fusion | flops 411025408 | bytes 17662976 | tf_op jit(solution)/shard_map/while/body/eval_jaxpr/mkj,mkr->mjr/dot_general | solution.py:13
  38.9 0.7 fusion.21
  39.6 16.3 %fusion.20 = (f32[32,512]{1,0:T(8,128)S(1)}, f32[32,256,512]{2,1,0:T(8,128)S(1)}) fusion(f32[8,32,8,512]{3,2,1,0:T(8,128)} %get-tuple-element.285, s32[]{:T(128)} %get-tuple-element.274, f32[8,32,8,256]{3,2,1,0:T(8,128)} %get-tuple-element.284, f32[32,256]{1,0:T(8,128)S(1)} %dynamic-slice_bitcast_fusion.4), kind=kOutput, calls=%fused_computation.30.clone.1 | convolution fusion | flops 411025408 | bytes 17662976 | tf_op jit(solution)/shard_map/while/body/eval_jaxpr/mkj,mkr->mjr/dot_general | solution.py:13
  56.7 16.3 %fusion.20 = (f32[32,512]{1,0:T(8,128)S(1)}, f32[32,256,512]{2,1,0:T(8,128)S(1)}) fusion(f32[8,32,8,512]{3,2,1,0:T(8,128)} %get-tuple-element.285, s32[]{:T(128)} %get-tuple-element.274, f32[8,32,8,256]{3,2,1,0:T(8,128)} %get-tuple-element.284, f32[32,256]{1,0:T(8,128)S(1)} %dynamic-slice_bitcast_fusion.4), kind=kOutput, calls=%fused_computation.30.clone.1 | convolution fusion | flops 411025408 | bytes 17662976 | tf_op jit(solution)/shard_map/while/body/eval_jaxpr/mkj,mkr->mjr/dot_general | solution.py:13
  73.7 16.3 %fusion.20 = (f32[32,512]{1,0:T(8,128)S(1)}, f32[32,256,512]{2,1,0:T(8,128)S(1)}) fusion(f32[8,32,8,512]{3,2,1,0:T(8,128)} %get-tuple-element.285, s32[]{:T(128)} %get-tuple-element.274, f32[8,32,8,256]{3,2,1,0:T(8,128)} %get-tuple-element.284, f32[32,256]{1,0:T(8,128)S(1)} %dynamic-slice_bitcast_fusion.4), kind=kOutput, calls=%fused_computation.30.clone.1 | convolution fusion | flops 411025408 | bytes 17662976 | tf_op jit(solution)/shard_map/while/body/eval_jaxpr/mkj,mkr->mjr/dot_general | solution.py:13
  90.8 16.3 %fusion.20 = (f32[32,512]{1,0:T(8,128)S(1)}, f32[32,256,512]{2,1,0:T(8,128)S(1)}) fusion(f32[8,32,8,512]{3,2,1,0:T(8,128)} %get-tuple-element.285, s32[]{:T(128)} %get-tuple-element.274, f32[8,32,8,256]{3,2,1,0:T(8,128)} %get-tuple-element.284, f32[32,256]{1,0:T(8,128)S(1)} %dynamic-slice_bitcast_fusion.4), kind=kOutput, calls=%fused_computation.30.clone.1 | convolution fusion | flops 411025408 | bytes 17662976 | tf_op jit(solution)/shard_map/while/body/eval_jaxpr/mkj,mkr->mjr/dot_general | solution.py:13
  107.9 16.3 %fusion.20 = (f32[32,512]{1,0:T(8,128)S(1)}, f32[32,256,512]{2,1,0:T(8,128)S(1)}) fusion(f32[8,32,8,512]{3,2,1,0:T(8,128)} %get-tuple-element.285, s32[]{:T(128)} %get-tuple-element.274, f32[8,32,8,256]{3,2,1,0:T(8,128)} %get-tuple-element.284, f32[32,256]{1,0:T(8,128)S(1)} %dynamic-slice_bitcast_fusion.4), kind=kOutput, calls=%fused_computation.30.clone.1 | convolution fusion | flops 411025408 | bytes 17662976 | tf_op jit(solution)/shard_map/while/body/eval_jaxpr/mkj,mkr->mjr/dot_general | solution.py:13
  125.0 16.3 %fusion.20 = (f32[32,512]{1,0:T(8,128)S(1)}, f32[32,256,512]{2,1,0:T(8,128)S(1)}) fusion(f32[8,32,8,512]{3,2,1,0:T(8,128)} %get-tuple-element.285, s32[]{:T(128)} %get-tuple-element.274, f32[8,32,8,256]{3,2,1,0:T(8,128)} %get-tuple-element.284, f32[32,256]{1,0:T(8,128)S(1)} %dynamic-slice_bitcast_fusion.4), kind=kOutput, calls=%fused_computation.30.clone.1 | convolution fusion | flops 411025408 | bytes 17662976 | tf_op jit(solution)/shard_map/while/body/eval_jaxpr/mkj,mkr->mjr/dot_general | solution.py:13
  142.0 16.3 %fusion.20 = (f32[32,512]{1,0:T(8,128)S(1)}, f32[32,256,512]{2,1,0:T(8,128)S(1)}) fusion(f32[8,32,8,512]{3,2,1,0:T(8,128)} %get-tuple-element.285, s32[]{:T(128)} %get-tuple-element.274, f32[8,32,8,256]{3,2,1,0:T(8,128)} %get-tuple-element.284, f32[32,256]{1,0:T(8,128)S(1)} %dynamic-slice_bitcast_fusion.4), kind=kOutput, calls=%fused_computation.30.clone.1 | convolution fusion | flops 411025408 | bytes 17662976 | tf_op jit(solution)/shard_map/while/body/eval_jaxpr/mkj,mkr->mjr/dot_general | solution.py:13
  159.8 43.5 %all-reduce.4.cloned.1.call-done = f32[256,128]{1,0:T(8,128)} async-done(((f32[256,128]{1,0:T(8,128)}), f32[256,128]{1,0:T(8,128)}) %all-reduce.4.cloned.1.call-update) | async-done | bytes 131088 | tf_op jit(solution)/shard_map/psum | solution.py:43
  203.4 0.9 log_subtract_fusion.1
  204.3 2.0 all_gather.11
  206.3 136.8 %while.25 = (s32[]{:T(128)}, f32[8,32,128]{2,1,0:T(8,128)S(1)}, f32[8,32,256]{2,1,0:T(8,128)S(1)}, f32[8,32,8,256]{3,2,1,0:T(8,128)}, f32[8,32,8,512]{3,2,1,0:T(8,128)}, /*index=5*/s32[]{:T(128)}, s32[]{:T(128)}) while((s32[]{:T(128)}, f32[8,32,128]{2,1,0:T(8,128)S(1)}, f32[8,32,256]{2,1,0:T(8,128)S(1)}, f32[8,32,8,256]{3,2,1,0:T(8,128)}, ...), condition=%wide.region_8.9_spmd, body=%wide.region_5.8_spmd.sunk | while | flops 415232000 | bytes 26362968 | solution.py:39
  206.5 16.3 %fusion.22 = (f32[32,512]{1,0:T(8,128)S(1)}, f32[32,256,512]{2,1,0:T(8,128)S(1)}) fusion(f32[8,32,8,512]{3,2,1,0:T(8,128)} %get-tuple-element.306, s32[]{:T(128)} %get-tuple-element.295, f32[8,32,8,256]{3,2,1,0:T(8,128)} %get-tuple-element.305, f32[32,256]{1,0:T(8,128)S(1)} %dynamic-slice_bitcast_fusion.5), kind=kOutput, calls=%fused_computation.31.clone.1 | convolution fusion | flops 411025408 | bytes 17662976 | tf_op jit(solution)/shard_map/while/body/eval_jaxpr/mkj,mkr->mjr/dot_general | solution.py:13
  223.6 16.3 %fusion.22 = (f32[32,512]{1,0:T(8,128)S(1)}, f32[32,256,512]{2,1,0:T(8,128)S(1)}) fusion(f32[8,32,8,512]{3,2,1,0:T(8,128)} %get-tuple-element.306, s32[]{:T(128)} %get-tuple-element.295, f32[8,32,8,256]{3,2,1,0:T(8,128)} %get-tuple-element.305, f32[32,256]{1,0:T(8,128)S(1)} %dynamic-slice_bitcast_fusion.5), kind=kOutput, calls=%fused_computation.31.clone.1 | convolution fusion | flops 411025408 | bytes 17662976 | tf_op jit(solution)/shard_map/while/body/eval_jaxpr/mkj,mkr->mjr/dot_general | solution.py:13
  240.7 16.3 %fusion.22 = (f32[32,512]{1,0:T(8,128)S(1)}, f32[32,256,512]{2,1,0:T(8,128)S(1)}) fusion(f32[8,32,8,512]{3,2,1,0:T(8,128)} %get-tuple-element.306, s32[]{:T(128)} %get-tuple-element.295, f32[8,32,8,256]{3,2,1,0:T(8,128)} %get-tuple-element.305, f32[32,256]{1,0:T(8,128)S(1)} %dynamic-slice_bitcast_fusion.5), kind=kOutput, calls=%fused_computation.31.clone.1 | convolution fusion | flops 411025408 | bytes 17662976 | tf_op jit(solution)/shard_map/while/body/eval_jaxpr/mkj,mkr->mjr/dot_general | solution.py:13
  257.7 16.3 %fusion.22 = (f32[32,512]{1,0:T(8,128)S(1)}, f32[32,256,512]{2,1,0:T(8,128)S(1)}) fusion(f32[8,32,8,512]{3,2,1,0:T(8,128)} %get-tuple-element.306, s32[]{:T(128)} %get-tuple-element.295, f32[8,32,8,256]{3,2,1,0:T(8,128)} %get-tuple-element.305, f32[32,256]{1,0:T(8,128)S(1)} %dynamic-slice_bitcast_fusion.5), kind=kOutput, calls=%fused_computation.31.clone.1 | convolution fusion | flops 411025408 | bytes 17662976 | tf_op jit(solution)/shard_map/while/body/eval_jaxpr/mkj,mkr->mjr/dot_general | solution.py:13
  274.1 0.7 fusion.23
  274.8 16.3 %fusion.22 = (f32[32,512]{1,0:T(8,128)S(1)}, f32[32,256,512]{2,1,0:T(8,128)S(1)}) fusion(f32[8,32,8,512]{3,2,1,0:T(8,128)} %get-tuple-element.306, s32[]{:T(128)} %get-tuple-element.295, f32[8,32,8,256]{3,2,1,0:T(8,128)} %get-tuple-element.305, f32[32,256]{1,0:T(8,128)S(1)} %dynamic-slice_bitcast_fusion.5), kind=kOutput, calls=%fused_computation.31.clone.1 | convolution fusion | flops 411025408 | bytes 17662976 | tf_op jit(solution)/shard_map/while/body/eval_jaxpr/mkj,mkr->mjr/dot_general | solution.py:13
  291.9 16.3 %fusion.22 = (f32[32,512]{1,0:T(8,128)S(1)}, f32[32,256,512]{2,1,0:T(8,128)S(1)}) fusion(f32[8,32,8,512]{3,2,1,0:T(8,128)} %get-tuple-element.306, s32[]{:T(128)} %get-tuple-element.295, f32[8,32,8,256]{3,2,1,0:T(8,128)} %get-tuple-element.305, f32[32,256]{1,0:T(8,128)S(1)} %dynamic-slice_bitcast_fusion.5), kind=kOutput, calls=%fused_computation.31.clone.1 | convolution fusion | flops 411025408 | bytes 17662976 | tf_op jit(solution)/shard_map/while/body/eval_jaxpr/mkj,mkr->mjr/dot_general | solution.py:13
  309.0 16.3 %fusion.22 = (f32[32,512]{1,0:T(8,128)S(1)}, f32[32,256,512]{2,1,0:T(8,128)S(1)}) fusion(f32[8,32,8,512]{3,2,1,0:T(8,128)} %get-tuple-element.306, s32[]{:T(128)} %get-tuple-element.295, f32[8,32,8,256]{3,2,1,0:T(8,128)} %get-tuple-element.305, f32[32,256]{1,0:T(8,128)S(1)} %dynamic-slice_bitcast_fusion.5), kind=kOutput, calls=%fused_computation.31.clone.1 | convolution fusion | flops 411025408 | bytes 17662976 | tf_op jit(solution)/shard_map/while/body/eval_jaxpr/mkj,mkr->mjr/dot_general | solution.py:13
  326.1 16.3 %fusion.22 = (f32[32,512]{1,0:T(8,128)S(1)}, f32[32,256,512]{2,1,0:T(8,128)S(1)}) fusion(f32[8,32,8,512]{3,2,1,0:T(8,128)} %get-tuple-element.306, s32[]{:T(128)} %get-tuple-element.295, f32[8,32,8,256]{3,2,1,0:T(8,128)} %get-tuple-element.305, f32[32,256]{1,0:T(8,128)S(1)} %dynamic-slice_bitcast_fusion.5), kind=kOutput, calls=%fused_computation.31.clone.1 | convolution fusion | flops 411025408 | bytes 17662976 | tf_op jit(solution)/shard_map/while/body/eval_jaxpr/mkj,mkr->mjr/dot_general | solution.py:13
  342.4 0.7 fusion.23
  343.8 42.4 %all-reduce.6.cloned.1.call-done = f32[256,128]{1,0:T(8,128)} async-done(((f32[256,128]{1,0:T(8,128)}), f32[256,128]{1,0:T(8,128)}) %all-reduce.6.cloned.1.call-update) | async-done | bytes 131088 | tf_op jit(solution)/shard_map/psum | solution.py:43
  386.2 2.2 multiply_reduce_fusion.1
  388.4 16.6 %all-reduce = (f32[1]{0:T(128)}, f32[1]{0:T(128)}) all-reduce(f32[1]{0:T(128)} %bitcast.15, f32[1]{0:T(128)} %bitcast.14), channel_id=1, replica_groups=mesh['mkt'=4,'prod'=2,'draw'=4] {'mkt','prod'}, use_global_device_ids=true, to_apply=%region_13.14 | all-reduce | flops 2 | bytes 16 | tf_op jit(solution)/shard_map/psum | solution.py:47
  405.0 1.8 fusion.13
  (76 shorter events, 10.6 us)
Async XLA Ops:
  7.2 15.2 %all-gather.2.cloned.1.call-start = ((), (), s32[]{:S(2)}) async-start(), calls=%async_computation | async-start | bytes 3145728 | tf_op jit(solution)/shard_map/all_gather | solution.py:24
  7.9 195.5 %all-reduce.4.cloned.1.call-start = ((), (), s32[]{:S(2)}) async-start(), calls=%async_computation.1 | async-start | bytes 262144 | tf_op jit(solution)/shard_map/psum | solution.py:43
  22.4 181.0 %copy-start = (f32[256,128]{1,0:T(8,128)S(1)}, f32[256,128]{1,0:T(8,128)}, u32[]{:S(2)}) copy-start(f32[256,128]{1,0:T(8,128)} %param.9) | copy-start | bytes 393220
  22.4 181.0 %copy-start.1 = (f32[256,128]{1,0:T(8,128)S(1)}, f32[256,128]{1,0:T(8,128)}, u32[]{:S(2)}) copy-start(f32[256,128]{1,0:T(8,128)} %param.10) | copy-start | bytes 393220
  159.1 0.7 copy-start.3
  159.8 226.4 %all-reduce.6.cloned.1.call-start = ((), (), s32[]{:S(2)}) async-start(), calls=%async_computation.2 | async-start | bytes 262144 | tf_op jit(solution)/shard_map/psum | solution.py:43
  343.1 0.7 copy-start.2
Sparse Core Ops, SparseCore 0:
  9.5 12.8 all-gather.1
  159.9 43.4 all-reduce.3
  343.9 42.1 all-reduce.5
where the time goes:
time: 414 us; the launch traced here: 413 us
  matrix products  261 us (63%)
  waiting for transfers between devices  94 us (23%)
  blocking collectives  20.9 us (5%)
  other arithmetic  20.5 us (5%)
  between operations  13.8 us (3%)
    dot_general x16, matrix products, exponent(): jnp.einsum('mkj,mkr->mjr', chars_part, scaled_part, precision=lax.Precisi...  261 us
    psum x2, waiting for transfers between devices, shards(): predicted = lax.psum(summed.reshape(markets, local_prod), 'draw') / R  85.9 us
    psum x1, blocking collectives, shards(): norm_list.append(lax.psum(square_sum, ('mkt', 'prod')))  16.6 us
    reduce_sum x16, other arithmetic, whole_pass(): return jnp.sum(own_part / denominator, axis=2)  10.7 us
  transfers between devices with their start and end apart: 3, of which 3 were waited for; matrix products, arithmetic and copies ran while one was open for 1% of the time, Pallas kernels for 0%

commit v1 on v0

v1 whole, which is shorter than its diff:
```python
import functools
import math

import jax
import jax.numpy as jnp
from jax import lax
from jax.experimental import pallas as pl
from jax.experimental.pallas import tpu as pltpu
from jax.sharding import PartitionSpec as P

ITERS = 2
UNROLL = 2
LOG2E = math.log2(math.e)
MESH = pl.DeviceIdType.MESH
F32, BF16 = jnp.float32, jnp.bfloat16


def split(x):
    high = x.astype(BF16).astype(F32)
    return high, x - high


def kernel(sizes, chunks, coef, start, shares, chars, tastes, out, norms, util, logs, cbuf, tbuf, pred, square,
           util_sem, char_sem, taste_sem, prod_send, prod_recv, sum_send, sum_recv, fin_local, fin_send, fin_recv,
           sq_send, sq_recv):
    n_mkt, n_prod, n_draw = sizes
    m, p, d = lax.axis_index("mkt"), lax.axis_index("prod"), lax.axis_index("draw")
    markets, coefs, width = chars.shape
    share = markets // n_prod
    rows_of = share // chunks
    products = width * n_prod
    draws = tbuf.shape[2]
    lane = min(draws, 128)

    def local_copies(c):
        rows = pl.ds(p * share + c * rows_of, rows_of)
        here = pl.ds(c * rows_of, rows_of)
        return (
            pltpu.make_async_copy(chars.at[rows], cbuf.at[0, here], char_sem.at[c]),
            pltpu.make_async_copy(tastes.at[rows], tbuf.at[here], taste_sem.at[c]),
        )

    mine = pl.ds(p * share, share)
    util_copies = [
        pltpu.make_async_copy(start.at[mine], util.at[:, pl.ds(0, width)], util_sem.at[0]),
        pltpu.make_async_copy(shares.at[mine], logs.at[:, pl.ds(0, width)], util_sem.at[1]),
    ]
    loads = [local_copies(c) for c in range(chunks)]
    for copy in util_copies:
        copy.start()
    for pair in loads:
        for copy in pair:
            copy.start()

    barrier = pltpu.get_barrier_semaphore()
    n_group = n_mkt * n_prod
    me = m * n_prod + p
    for k in range(1, n_group):
        t = lax.rem(me + k, n_group)
        pl.semaphore_signal(barrier, inc=1, device_id=(t // n_prod, lax.rem(t, n_prod), d), device_id_type=MESH)
    for k in range(1, n_draw):
        pl.semaphore_signal(barrier, inc=1, device_id=(m, p, lax.rem(d + k, n_draw)), device_id_type=MESH)
    pl.semaphore_wait(barrier, n_group - 1 + n_draw - 1)

    util_sends, char_sends = [], [[] for _ in range(chunks)]
    for o in range(1, n_prod):
        q = lax.rem(p + o, n_prod)
        target = (m, q, d)
        theirs = pl.ds(q * share, share)
        for i, (src, dst) in enumerate(((start, util), (shares, logs))):
            util_sends.append(pltpu.make_async_remote_copy(
                src.at[theirs], dst.at[:, pl.ds(o * width, width)],
                prod_send.at[chunks + i, o - 1], prod_recv.at[chunks + i, o - 1], device_id=target, device_id_type=MESH))
        for c in range(chunks):
            char_sends[c].append(pltpu.make_async_remote_copy(
                chars.at[pl.ds(q * share + c * rows_of, rows_of)], cbuf.at[o, pl.ds(c * rows_of, rows_of)],
                prod_send.at[c, o - 1], prod_recv.at[c, o - 1], device_id=target, device_id_type=MESH))
    for copy in util_sends:
        copy.start()
    for group in char_sends:
        for copy in group:
            copy.start()

    row_id = lax.broadcasted_iota(jnp.int32, (coefs, width), 0)
    scale = jnp.zeros((coefs, width), F32)
    for k in range(coefs):
        scale = jnp.where(row_id == k, coef[k], scale)
    scale = scale * LOG2E
    urow = lax.broadcasted_iota(jnp.int32, (8, products), 0)
    ones = jnp.ones((16, 2 * lane), BF16)
    plain = jnp.ones((8, draws), F32)

    def market(step, c, i):
        row = c * rows_of + i
        c_high, c_low = split(jnp.concatenate([cbuf[o, row] * scale for o in range(n_prod)], axis=1))
        s_high, s_low = split(tbuf[row])
        u = jnp.broadcast_to(util[pl.ds(row, 1), :] * LOG2E, (8, products))
        u_high, rest = split(u)
        u_mid, u_low = split(rest)
        u_part = jnp.where(urow == 0, u_high, jnp.where(urow == 1, u_mid, jnp.where(urow == 2, u_low, 0.0)))
        left = jnp.concatenate([c_high, c_low, c_high, u_part], axis=0).astype(BF16)
        right = jnp.concatenate([s_high, s_high, s_low, plain], axis=0).astype(BF16)
        total = jnp.zeros((products, lane), F32)
        block = min(draws, 256)
        for b in range(draws // block):
            power = lax.dot_general(left, right[:, b * block:(b + 1) * block], (((0,), (0,)), ((), ())),
                                    preferred_element_type=F32)
            for a in range(block // lane):
                weight = jnp.exp2(power[:, a * lane:(a + 1) * lane])
                inverse = 1.0 / (1.0 + jnp.sum(weight, axis=0, keepdims=True))
                total = total + weight * inverse
        t_high, t_low = split(total)
        both = jnp.concatenate([t_high.astype(BF16), t_low.astype(BF16)], axis=1)
        summed = lax.dot_general(ones, both, (((1,), (1,)), ((), ())), preferred_element_type=F32)
        pred[step, c, d, pl.ds(i, 1), :] = summed[0:1]

    def predict(step, c):
        def body(i, carry):
            for j in range(UNROLL):
                market(step, c, i * UNROLL + j)
            return carry

        lax.fori_loop(0, rows_of // UNROLL, body, 0)

    def sum_copies(step, c):
        return [pltpu.make_async_remote_copy(
            pred.at[step, c, d], pred.at[step, c, d], sum_send.at[step, c, o - 1], sum_recv.at[step, c, o - 1],
            device_id=(m, p, lax.rem(d + o, n_draw)), device_id_type=MESH) for o in range(1, n_draw)]

    pending = {}

    def send_sums(step, c):
        pending[step, c] = sum_copies(step, c)
        for copy in pending[step, c]:
            copy.start()

    parts = [jnp.zeros((8, 128), F32) for _ in range(ITERS)]

    def update(step, c):
        for copy in pending[step, c]:
            copy.wait()
        rows = pl.ds(c * rows_of, rows_of)
        total = pred[step, c, 0]
        for s in range(1, n_draw):
            total = total + pred[step, c, s]
        old = util[rows, :]
        new = old + logs[rows, :] - jnp.log(total / (draws * n_draw))
        change = new - old
        util[rows, :] = new
        change = change * change
        for a in range(rows_of // 8):
            for b in range(products // 128):
                parts[step] = parts[step] + change[a * 8:(a + 1) * 8, b * 128:(b + 1) * 128]

    finals = []

    def finish(c):
        here = pl.ds(c * rows_of, rows_of)
        rows = pl.ds(p * share + c * rows_of, rows_of)
        copy = pltpu.make_async_copy(util.at[here, pl.ds(0, width)], out.at[rows], fin_local.at[c])
        copy.start()
        finals.append(copy)
        for o in range(1, n_prod):
            copy = pltpu.make_async_remote_copy(
                util.at[here, pl.ds(o * width, width)], out.at[rows], fin_send.at[c, o - 1], fin_recv.at[c, o - 1],
                device_id=(m, lax.rem(p + n_prod - o, n_prod), d), device_id_type=MESH)
            copy.start()
            finals.append(copy)

    for copy in util_copies + util_sends:
        copy.wait()
    for c in range(chunks):
        for copy in [*loads[c], *char_sends[c]]:
            copy.wait()
        predict(0, c)
        send_sums(0, c)
    for step in range(1, ITERS):
        for c in range(chunks):
            update(step - 1, c)
            predict(step, c)
            send_sums(step, c)
    for c in range(chunks):
        update(ITERS - 1, c)
        finish(c)

    for step in range(ITERS):
        square[me, step] = parts[step]
    copies = []
    for k in range(1, n_group):
        t = lax.rem(me + k, n_group)
        copies.append(pltpu.make_async_remote_copy(
            square.at[me], square.at[me], sq_send.at[k - 1], sq_recv.at[k - 1],
            device_id=(t // n_prod, lax.rem(t, n_prod), d), device_id_type=MESH))
    for copy in copies:
        copy.start()
    for copy in copies:
        copy.wait()
    cells = markets * n_mkt * products
    for step in range(ITERS):
        total = square[0, step]
        for k in range(1, n_group):
            total = total + square[k, step]
        mean = jnp.full((8, 128), jnp.sum(total) / cells + 1e-06, F32)
        norms[step] = jnp.max(jnp.sqrt(mean))
    for copy in finals:
        copy.wait()


def solution(mesh):
    sizes = tuple(mesh.shape[name] for name in ("mkt", "prod", "draw"))
    n_mkt, n_prod, n_draw = sizes

    def shards(start_utility, log_shares, characteristics, coef_scale, taste_draws):
        markets, coefs, width = characteristics.shape
        draws = taste_draws.shape[2]
        share = markets // n_prod
        chunks = math.gcd(share // 8, 4)
        rows_of = share // chunks
        products = width * n_prod
        dma = pltpu.SemaphoreType.DMA
        pairs = n_prod - 1
        anywhere = pl.BlockSpec(memory_space=pl.ANY)
        return pl.pallas_call(
            functools.partial(kernel, sizes, chunks),
            out_shape=(jax.ShapeDtypeStruct((markets, width), F32), jax.ShapeDtypeStruct((ITERS,), F32)),
            in_specs=[pl.BlockSpec(memory_space=pltpu.SMEM)] + [anywhere] * 4,
            out_specs=(anywhere, pl.BlockSpec(memory_space=pltpu.SMEM)),
            scratch_shapes=[
                pltpu.VMEM((share, products), F32),
                pltpu.VMEM((share, products), F32),
                pltpu.VMEM((n_prod, share, coefs, width), F32),
                pltpu.VMEM((share, coefs, draws), F32),
                pltpu.VMEM((ITERS, chunks, n_draw, rows_of, products), F32),
                pltpu.VMEM((n_mkt * n_prod, ITERS, 8, 128), F32),
                dma((2,)), dma((chunks,)), dma((chunks,)),
                dma((chunks + 2, pairs)), dma((chunks + 2, pairs)),
                dma((ITERS, chunks, n_draw - 1)), dma((ITERS, chunks, n_draw - 1)),
                dma((chunks,)), dma((chunks, pairs)), dma((chunks, pairs)),
                dma((n_mkt * n_prod - 1,)), dma((n_mkt * n_prod - 1,)),
            ],
            compiler_params=pltpu.CompilerParams(collective_id=0, has_side_effects=True),
        )(coef_scale, start_utility, log_shares, characteristics, taste_draws)

    return jax.shard_map(
        shards,
        mesh=mesh,
        in_specs=(P("mkt", "prod"), P("mkt", "prod"), P("mkt", None, "prod"), P(), P("mkt", None, "draw")),
        out_specs=(P("mkt", "prod"), P()),
        check_vma=False,
    )
```

time: 414 us -> 120 us (0.29)
  matrix products: 261 us -> 0 us
  Pallas kernels: 0 us -> 117 us
  waiting for transfers between devices: 94 us -> 0 us
  blocking collectives: 20.9 us -> 0 us
  other arithmetic: 20.5 us -> 0 us
  between operations: 13.8 us -> 0.64 us
    dot_general x16 -> x0, matrix products: 261 us -> none  [exponent(): jnp.einsum('mkj,mkr->mjr', chars_part, scaled_part, precision=lax.Precisi...]
    pallas_call x0 -> x1, Pallas kernels: none -> 117 us  [shards(): pl.pallas_call(functools.partial(kernel, sizes, chunks), out_shape=(jax.S...]
    psum x2 -> x0, waiting for transfers between devices: 85.9 us -> none  [shards(): predicted = lax.psum(summed.reshape(markets, local_prod), 'draw') / R]
    psum x1 -> x0, blocking collectives: 16.6 us -> none  [shards(): norm_list.append(lax.psum(square_sum, ('mkt', 'prod')))]
    reduce_sum x17 -> x0, other arithmetic: 12.9 us -> none  [the longest x16 10.7 us: whole_pass(): return jnp.sum(own_part / denominator, axis=2)]
    all_gather x1 -> x0, waiting for transfers between devices: 7.39 us -> none  [shards(): all_chars = lax.all_gather(characteristics, 'prod', axis=2, tiled=True)]
    mul x1 -> x0, other arithmetic: 4.69 us -> none  [shards(): scaled = taste_draws * coef_scale[None, :, None]]
    all_gather x2 -> x0, blocking collectives: 4.33 us -> none  [shards(): full_utility = lax.all_gather(utility, 'prod', axis=1, tiled=True)]
  transfers between devices with their start and end apart: 3 -> 0, of which waited for: 3 -> 0; matrix products, arithmetic and copies ran while one was open for 1% -> 0% of each run, Pallas kernels for 0% -> 0%
where the time goes in v1:
time: 120 us
  Pallas kernels  117 us (98%)
  local copies, waits for them, and re-layouts  2.74 us (2%)
    pallas_call x1, Pallas kernels, shards(): pl.pallas_call(functools.partial(kernel, sizes, chunks), out_shape=(jax.S...  117 us
    unnamed x2, local copies, waits for them, and re-layouts  2.74 us

profile of v1, /device:TPU:0, one launch (start us, length us, event | category | flops | bytes accessed | tf_op | source)
XLA Modules:
  0.0 119.9 jit_solution(10634650316190265078)
XLA Ops:
  0.6 116.5 %shard_map.68 = (f32[256,128]{1,0:T(8,128)}, f32[2]{0:T(128)}) custom-call(f32[8]{0:T(128)} %coef.1, f32[256,128]{1,0:T(8,128)} %start.1, f32[256,128]{1,0:T(8,128)} %shares.1, f32[256,8,128]{2,1,0:T(8,128)} %chars.1, f32[256,8,512]{2,1,0:T(8,128)} %tastes.1), custom_call_target="tpu_custom_call" | custom-call | tf_op jit(solution)/shard_map/pallas_call | solution.py:223
  117.2 1.6 %copy.9 = f32[256,128]{1,0:T(8,128)} copy(f32[256,128]{1,0:T(8,128)} %get-tuple-element.4) | data formatting | bytes 262144
  118.7 1.2 copy.10

commit v2 on v1

--- a/solution.py
+++ b/solution.py
@@ -9,7 +9,7 @@
 from jax.sharding import PartitionSpec as P
 
 ITERS = 2
-UNROLL = 2
+UNROLL = 8
 LOG2E = math.log2(math.e)
 MESH = pl.DeviceIdType.MESH
 F32, BF16 = jnp.float32, jnp.bfloat16
@@ -20,7 +20,7 @@
     return high, x - high
 
 
-def kernel(sizes, chunks, coef, start, shares, chars, tastes, out, norms, util, logs, cbuf, tbuf, pred, square,
+def kernel(sizes, chunks, coef, start, shares, chars, tastes, out, norms, util, logs, cbuf, tbuf, pred, square, turned,
            util_sem, char_sem, taste_sem, prod_send, prod_recv, sum_send, sum_recv, fin_local, fin_send, fin_recv,
            sq_send, sq_recv):
     n_mkt, n_prod, n_draw = sizes
@@ -87,7 +87,8 @@
         scale = jnp.where(row_id == k, coef[k], scale)
     scale = scale * LOG2E
     urow = lax.broadcasted_iota(jnp.int32, (8, products), 0)
-    ones = jnp.ones((16, 2 * lane), BF16)
+    column = lax.broadcasted_iota(jnp.int32, turned.shape, 1)
+    turned[...] = jnp.zeros(turned.shape, F32)
     plain = jnp.ones((8, draws), F32)
 
     def market(step, c, i):
@@ -109,18 +110,19 @@
                 weight = jnp.exp2(power[:, a * lane:(a + 1) * lane])
                 inverse = 1.0 / (1.0 + jnp.sum(weight, axis=0, keepdims=True))
                 total = total + weight * inverse
-        t_high, t_low = split(total)
-        both = jnp.concatenate([t_high.astype(BF16), t_low.astype(BF16)], axis=1)
-        summed = lax.dot_general(ones, both, (((1,), (1,)), ((), ())), preferred_element_type=F32)
-        pred[step, c, d, pl.ds(i, 1), :] = summed[0:1]
+        return jnp.sum(total, axis=1, keepdims=True)
 
     def predict(step, c):
         def body(i, carry):
+            sums = [market(step, c, i * UNROLL + j) for j in range(UNROLL)]
+            held = turned[...]
             for j in range(UNROLL):
-                market(step, c, i * UNROLL + j)
+                held = jnp.where(column == i * UNROLL + j, sums[j], held)
+            turned[...] = held
             return carry
 
         lax.fori_loop(0, rows_of // UNROLL, body, 0)
+        pred[step, c, d] = turned[...].T[0:rows_of]
 
     def sum_copies(step, c):
         return [pltpu.make_async_remote_copy(
@@ -232,6 +234,7 @@
                 pltpu.VMEM((share, coefs, draws), F32),
                 pltpu.VMEM((ITERS, chunks, n_draw, rows_of, products), F32),
                 pltpu.VMEM((n_mkt * n_prod, ITERS, 8, 128), F32),
+                pltpu.VMEM((products, 128), F32),
                 dma((2,)), dma((chunks,)), dma((chunks,)),
                 dma((chunks + 2, pairs)), dma((chunks + 2, pairs)),
                 dma((ITERS, chunks, n_draw - 1)), dma((ITERS, chunks, n_draw - 1)),

time: 120 us -> 52.5 us (0.44)
  Pallas kernels: 117 us -> 49 us
    pallas_call x1, Pallas kernels: 117 us -> 49 us  [shards(): pl.pallas_call(functools.partial(kernel, sizes, chunks), out_shape=(jax.S...]
where the time goes in v2:
time: 52.5 us; the launch traced here: 52.4 us
  Pallas kernels  49 us (93%)
  local copies, waits for them, and re-layouts  2.74 us (5%)
  between operations  0.64 us (1%)
    pallas_call x1, Pallas kernels, shards(): pl.pallas_call(functools.partial(kernel, sizes, chunks), out_shape=(jax.S...  49 us
    unnamed x2, local copies, waits for them, and re-layouts  2.74 us

profile of v2, /device:TPU:0, one launch (start us, length us, event | category | flops | bytes accessed | tf_op | source)
XLA Modules:
  0.0 52.4 jit_solution(2097318326067343738)
XLA Ops:
  0.6 49.0 %shard_map.68 = (f32[256,128]{1,0:T(8,128)}, f32[2]{0:T(128)}) custom-call(f32[8]{0:T(128)} %coef.1, f32[256,128]{1,0:T(8,128)} %start.1, f32[256,128]{1,0:T(8,128)} %shares.1, f32[256,8,128]{2,1,0:T(8,128)} %chars.1, f32[256,8,512]{2,1,0:T(8,128)} %tastes.1), custom_call_target="tpu_custom_call" | custom-call | tf_op jit(solution)/shard_map/pallas_call | solution.py:225
  49.6 1.6 %copy.9 = f32[256,128]{1,0:T(8,128)} copy(f32[256,128]{1,0:T(8,128)} %get-tuple-element.4) | data formatting | bytes 262144
  51.2 1.2 %copy.10 = f32[2]{0:T(128)} copy(f32[2]{0:T(128)} %get-tuple-element.5) | data formatting | bytes 16
